TPU v7x, 128 devices: a whole 4x4x4 slice. The times are simulated.
128 devices in a mesh: section: 2 (over core), dev: 64 (over x, z, y).
Axes of the slice: x: 4, y: 4, z: 4, core: 2. Of those that a mesh axis runs over, the one named last changes fastest.
Arguments:
- indices: int32 [8192, 32, 8], P(('section', 'dev')), may hold values from 0 to 131071
- pool_len: int32 [32], replicated, may hold values from 1 to 8
- tables: bfloat16 [4194304, 128], P(('section', 'dev')), may hold values from -3 to 3
- w_first: bfloat16 [4096, 4096], P('dev', 'section'), may hold values from -0.09375 to 0.09375
- b_first: bfloat16 [4096], P('section'), may hold values from -3 to 3
- w_out: bfloat16 [4096], P('section'), may hold values from -0.09375 to 0.09375
Outputs:
- logits: float32 [8192], P('dev')
Inputs may be any that keep to these rules, and one draw needn't show every extreme that they name: `indices`: ids of rows of the table named by the second index.
All inputs are finite; a program needn't handle non-finite values.
Results may differ from a plain program's by a relative error of at most 0.0095.
Values may be sent and summed in bfloat16 or wider, within the bound.
No kernel may reach another device: no remote copies, remote signals or barrier semaphores. Data moves between devices by JAX's collectives and lax.ppermute only.
A program may use at most 128 MiB of HBM per device.

v0:
```python
import jax
import jax.numpy as jnp
from jax import lax
from jax.sharding import PartitionSpec as P


def sent_to_all(shard, axis):
    devices = lax.axis_size(axis)
    return lax.all_to_all(
        jnp.broadcast_to(shard[None], (devices, *shard.shape)), axis, 0, 0, tiled=True
    )


def in_order(tiles, dim):
    shape = list(tiles.shape[1:])
    shape[dim] *= tiles.shape[0]
    return jnp.moveaxis(tiles, 0, dim).reshape(shape)


def collect(shard, axis, dim):
    tiles = sent_to_all(shard, axis)
    return in_order(tiles, dim)


def gathered_total(shard, axis):
    return lax.all_gather(shard, axis).sum(0)


def body(indices, pool_len, tables, w_first, b_first, w_out):
    sec_count = lax.axis_size("section")
    dev_count = lax.axis_size("dev")
    devices = sec_count * dev_count
    dev_rows, n_tables, pool_size = indices.shape
    rows_dev, emb_width = tables.shape
    row_split = devices // n_tables
    position = lax.axis_index("section") * dev_count + lax.axis_index("dev")
    table_id = position // row_split
    first_row = position % row_split * rows_dev
    outgoing = jnp.repeat(indices, row_split, axis=1)
    arrived = lax.all_to_all(outgoing, ("section", "dev"), split_axis=1, concat_axis=0, tiled=True)
    all_rows = devices * dev_rows
    wanted = arrived.reshape(all_rows, pool_size) - first_row
    live_slots = jnp.sum(jnp.where(jnp.arange(n_tables) == table_id, pool_len, 0))
    usable = (wanted >= 0) & (wanted < rows_dev) & (jnp.arange(pool_size)[None, :] < live_slots)
    safe_rows = jnp.where(usable, wanted, 0)
    looked = jnp.take(tables, safe_rows, axis=0)
    picked = jnp.where(usable[:, :, None], looked, jnp.zeros((), jnp.bfloat16))
    partial_value = jnp.sum(picked.astype(jnp.float32), axis=1).astype(jnp.bfloat16)
    ordered = jnp.transpose(
        partial_value.reshape(dev_count, sec_count, dev_rows, emb_width), (1, 0, 2, 3)
    )
    received = lax.all_to_all(
        ordered.reshape(devices, dev_rows, emb_width),
        ("section", "dev"),
        split_axis=0,
        concat_axis=0,
        tiled=True,
    )
    summed = jnp.sum(
        received.reshape(n_tables, row_split, dev_rows, emb_width).astype(jnp.float32), axis=1
    )
    features = jnp.transpose(summed.astype(jnp.bfloat16), (1, 0, 2)).reshape(
        dev_rows, n_tables * emb_width
    )
    samples = collect(features, "section", 0)
    whole_weights = lax.all_gather(w_first, "dev", axis=0, tiled=True)
    pre_act = jnp.dot(samples, whole_weights, preferred_element_type=jnp.float32)
    hidden = jnp.maximum(pre_act + b_first.astype(jnp.float32)[None, :], 0.0)
    logit_part = jnp.sum(hidden * w_out.astype(jnp.float32)[None, :], axis=1)
    return gathered_total(logit_part, "section")


def solution(mesh):
    placed = (
        P(("section", "dev"), None, None),
        P(),
        P(("section", "dev"), None),
        P("dev", "section"),
        P("section"),
        P("section"),
    )
    return jax.shard_map(body, mesh=mesh, in_specs=placed, out_specs=P("dev"), check_vma=False)
```

profile of v0, /device:TPU:1, one launch (start us, length us, event | category | flops | bytes accessed | tf_op | source)
XLA Modules:
  0.0 371.7 jit_solution(8074114564195128807)
XLA Ops:
  6.5 0.0 all-gather.4.cloned.1.call-start
  6.5 0.7 all-gather.4.cloned.1.call-update
  7.3 0.9 broadcast_in_dim.42
  8.2 1.0 reshape.131
  9.2 11.5 %all-to-all-start = ((s32[128,1,512]{2,1,0:T(1,128)}), s32[128,1,512]{2,1,0:T(1,128)S(1)}, u32[]{:S(2)}, u32[]{:S(2)}) async-start(s32[128,1,512]{2,1,0:T(1,128)} %reshape.131), calls=%async_computation | async-start | bytes 524288 | tf_op jit(solution)/shard_map/all_to_all | solution.py:40
  20.7 1.3 fusion.5
  22.0 0.6 iota_compare_fusion
  22.7 8.8 %all-to-all-done = s32[128,1,512]{2,1,0:T(1,128)S(1)} async-done(((s32[128,1,512]{2,1,0:T(1,128)}), s32[128,1,512]{2,1,0:T(1,128)S(1)}, u32[]{:S(2)}, u32[]{:S(2)}) %all-to-all-start) | async-done | bytes 262176 | tf_op jit(solution)/shard_map/all_to_all | solution.py:40
  31.5 0.5 broadcast.117
  32.0 1.3 reduce.3
  33.3 0.1 reshape.132
  33.5 0.1 copy.13
  33.6 0.2 sub.42
  33.8 0.2 sub.40
  33.9 0.1 compare_select_fusion
  34.1 2.6 copy.17
  36.6 3.6 reshape.120
  40.3 0.2 and_and_fusion
  40.5 1.7 copy.14
  42.2 1.7 copy.15
  43.9 222.4 %gather_fusion = bf16[65536,128]{1,0:T(8,128)(2,1)} fusion(bf16[32768,128]{1,0:T(8,128)(2,1)} %param.8, s32[65536]{0:T(1024)S(1)} %broadcast_clamp_fusion), kind=kCustom, calls=%fused_computation | custom fusion | bytes 33816576 | tf_op jit(solution)/shard_map/jit(_take)/gather | solution.py:46
  266.3 0.0 copy-start
  266.3 0.0 copy-start.1
  266.3 46.4 %fusion.1 = bf16[8192,128]{1,0:T(8,128)(2,1)S(1)} fusion(bf16[65536,128]{1,0:T(8,128)(2,1)} %gather_fusion, pred[8192,8]{1,0:T(8,128)(4,1)S(1)} %copy.15, pred[8192,8]{1,0:T(8,128)(4,1)S(1)} %copy.14), kind=kLoop, calls=%fused_computation.3 | loop fusion | flops 24117248 | bytes 19005440 | tf_op jit(solution)/shard_map/reduce_sum | solution.py:48
  312.7 1.5 copy.18
  314.2 4.3 %all-to-all-start.1 = ((bf16[128,64,128]{2,1,0:T(8,128)(2,1)}), bf16[128,64,128]{2,1,0:T(8,128)(2,1)S(1)}, u32[]{:S(2)}, u32[]{:S(2)}) async-start(bf16[128,64,128]{2,1,0:T(8,128)(2,1)} %bitcast.41), calls=%async_computation.1 | async-start | bytes 4194304 | tf_op jit(solution)/shard_map/all_to_all | solution.py:52
  318.5 0.0 copy-done
  318.5 0.0 copy-done.1
  318.5 30.1 %all-to-all-done.1 = bf16[128,64,128]{2,1,0:T(8,128)(2,1)S(1)} async-done(((bf16[128,64,128]{2,1,0:T(8,128)(2,1)}), bf16[128,64,128]{2,1,0:T(8,128)(2,1)S(1)}, u32[]{:S(2)}, u32[]{:S(2)}) %all-to-all-start.1) | async-done | bytes 2097184 | tf_op jit(solution)/shard_map/all_to_all | solution.py:52
  348.6 0.4 bitcast_reduce_fusion
  348.9 0.1 copy_bitcast_fusion
  349.0 0.1 broadcast_in_dim.49
  349.1 5.1 %all_to_all.19 = bf16[2,64,4096]{2,1,0:T(8,128)(2,1)S(1)} all-to-all(bf16[2,64,4096]{2,1,0:T(8,128)(2,1)S(1)} %broadcast_in_dim.49), channel_id=1, replica_groups=mesh['section'=2,'dev'=64] {'section'}, dimensions={0} | all-to-all | bytes 2097152 | tf_op jit(solution)/shard_map/all_to_all | solution.py:9
  354.3 0.0 all-gather.4.cloned.1.call-done
  354.3 8.2 %fusion.4 = f32[128]{0:T(128)S(1)} fusion(bf16[128,4096]{1,0:T(8,128)(2,1)S(1)} %bitcast.42, bf16[4096,2048]{1,0:T(8,128)(2,1)} %all-gather.4.cloned.1.call-done, f32[2048]{0:T(1024)S(1)} %convert_element_type.5, f32[2048]{0:T(1024)S(1)} %convert_element_type.4), kind=kOutput, calls=%fused_computation.8 | convolution fusion | flops 2148532224 | bytes 17842688 | tf_op jit(solution)/shard_map/dot_general | solution.py:67
  362.5 1.8 all-gather.1
  364.3 0.5 reduce_sum.55
  (4 shorter events, 0.1 us)
Async XLA Ops:
  6.5 347.7 %all-gather.4.cloned.1.call-start = ((), (), s32[]{:S(2)}) async-start(), calls=%async_computation.3 | async-start | bytes 17039360 | tf_op jit(solution)/shard_map/all_gather | solution.py:66
  9.2 22.3 %all-to-all-start = ((s32[128,1,512]{2,1,0:T(1,128)}), s32[128,1,512]{2,1,0:T(1,128)S(1)}, u32[]{:S(2)}, u32[]{:S(2)}) async-start(s32[128,1,512]{2,1,0:T(1,128)} %reshape.131), calls=%async_computation | async-start | bytes 524288 | tf_op jit(solution)/shard_map/all_to_all | solution.py:40
  266.3 52.2 %copy-start = (bf16[2048]{0:T(1024)(128)(2,1)S(1)}, bf16[2048]{0:T(1024)(128)(2,1)}, u32[]{:S(2)}) copy-start(bf16[2048]{0:T(1024)(128)(2,1)} %param.10) | copy-start | bytes 12292
  266.3 52.2 %copy-start.1 = (bf16[2048]{0:T(1024)(128)(2,1)S(1)}, bf16[2048]{0:T(1024)(128)(2,1)}, u32[]{:S(2)}) copy-start(bf16[2048]{0:T(1024)(128)(2,1)} %param.11) | copy-start | bytes 12292
  314.2 34.4 %all-to-all-start.1 = ((bf16[128,64,128]{2,1,0:T(8,128)(2,1)}), bf16[128,64,128]{2,1,0:T(8,128)(2,1)S(1)}, u32[]{:S(2)}, u32[]{:S(2)}) async-start(bf16[128,64,128]{2,1,0:T(8,128)(2,1)} %bitcast.41), calls=%async_computation.1 | async-start | bytes 4194304 | tf_op jit(solution)/shard_map/all_to_all | solution.py:52
Sparse Core Ops, SparseCore 0:
  10.2 107.0 all-gather.3
where the time goes:
time: 372 us
  local copies, waits for them, and re-layouts  237 us (64%)
  other arithmetic  50.9 us (14%)
  waiting for transfers between devices  39.6 us (11%)
  starting transfers between devices  15.8 us (4%)
  between operations  13.6 us (4%)
  matrix products  8.24 us (2%)
  blocking collectives  6.93 us (2%)
    gather x1, local copies, waits for them, and re-layouts, body(): looked = jnp.take(tables, safe_rows, axis=0)  222 us
    reduce_sum x1, other arithmetic, body(): jnp.sum(picked.astype(jnp.float32), axis=1).astype(jnp.bfloat16)  46.4 us
    all_to_all x1, waiting for transfers between devices, body(): lax.all_to_all(ordered.reshape(devices, dev_rows, emb_width), ('section',...  30.1 us
    all_to_all x1, starting transfers between devices, body(): lax.all_to_all(outgoing, ('section', 'dev'), split_axis=1, concat_axis=0,...  11.5 us
    all_to_all x1, waiting for transfers between devices, body(): lax.all_to_all(outgoing, ('section', 'dev'), split_axis=1, concat_axis=0,...  8.81 us
    dot_general x1, matrix products, body(): jnp.dot(samples, whole_weights, preferred_element_type=jnp.float32)  8.24 us
  transfers between devices with their start and end apart: 3, of which 2 were waited for; matrix products, arithmetic and copies ran while one was open for 77% of the time, Pallas kernels for 0%

commit v1 on v0

--- a/solution.py
+++ b/solution.py
@@ -37,7 +37,15 @@
     table_id = position // row_split
     first_row = position % row_split * rows_dev
     outgoing = jnp.repeat(indices, row_split, axis=1)
-    arrived = lax.all_to_all(outgoing, ("section", "dev"), split_axis=1, concat_axis=0, tiled=True)
+    arrived = jnp.concatenate(
+        lax.all_to_all(
+            jnp.stack(jnp.split(outgoing, lax.axis_size(("section", "dev")), axis=1)),
+            ("section", "dev"),
+            0,
+            0,
+        ),
+        axis=0,
+    )
     all_rows = devices * dev_rows
     wanted = arrived.reshape(all_rows, pool_size) - first_row
     live_slots = jnp.sum(jnp.where(jnp.arange(n_tables) == table_id, pool_len, 0))

time: 372 us -> 374 us (level)
  no operation moved by 1% of the time
where the time goes in v1:
time: 374 us
  local copies, waits for them, and re-layouts  237 us (63%)
  other arithmetic  50.9 us (14%)
  waiting for transfers between devices  39.6 us (11%)
  starting transfers between devices  16.6 us (4%)
  between operations  14.6 us (4%)
  matrix products  8.24 us (2%)
  blocking collectives  6.93 us (2%)
    gather x1, local copies, waits for them, and re-layouts, body(): looked = jnp.take(tables, safe_rows, axis=0)  222 us
    reduce_sum x1, other arithmetic, body(): jnp.sum(picked.astype(jnp.float32), axis=1).astype(jnp.bfloat16)  46.4 us
    all_to_all x1, waiting for transfers between devices, body(): lax.all_to_all(ordered.reshape(devices, dev_rows, emb_width), ('section',...  30.1 us
    all_to_all x1, starting transfers between devices, body(): lax.all_to_all(jnp.stack(jnp.split(outgoing, lax.axis_size(('section', 'd...  11.5 us
    all_to_all x1, waiting for transfers between devices, body(): lax.all_to_all(jnp.stack(jnp.split(outgoing, lax.axis_size(('section', 'd...  8.8 us
    dot_general x1, matrix products, body(): jnp.dot(samples, whole_weights, preferred_element_type=jnp.float32)  8.24 us
  transfers between devices with their start and end apart: 3, of which 2 were waited for; matrix products, arithmetic and copies ran while one was open for 77% of the time, Pallas kernels for 0%

profile of v1, /device:TPU:1, one launch (start us, length us, event | category | flops | bytes accessed | tf_op | source)
XLA Modules:
  0.0 374.0 jit_solution(17397200164476821890)
XLA Ops:
  6.5 0.0 all-gather.4.cloned.1.call-start
  6.5 0.7 all-gather.4.cloned.1.call-update
  7.3 0.9 broadcast_in_dim.42
  9.6 1.0 reshape.125
  10.6 11.5 %all-to-all-start = ((s32[128,1,512]{2,1,0:T(1,128)}), s32[128,1,512]{2,1,0:T(1,128)S(1)}, u32[]{:S(2)}, u32[]{:S(2)}) async-start(s32[128,1,512]{2,1,0:T(1,128)} %reshape.125), calls=%async_computation | async-start | bytes 524288 | tf_op jit(solution)/shard_map/all_to_all | solution.py:41
  22.1 1.3 fusion.5
  23.4 0.7 iota_compare_fusion
  24.1 8.8 %all-to-all-done = s32[128,1,512]{2,1,0:T(1,128)S(1)} async-done(((s32[128,1,512]{2,1,0:T(1,128)}), s32[128,1,512]{2,1,0:T(1,128)S(1)}, u32[]{:S(2)}, u32[]{:S(2)}) %all-to-all-start) | async-done | bytes 262176 | tf_op jit(solution)/shard_map/all_to_all | solution.py:41
  32.9 0.5 broadcast.109
  33.4 1.3 reduce.3
  34.7 0.1 reshape.126
  34.8 0.2 copy.666
  35.1 0.2 copy.667
  35.3 0.2 sub.32
  35.5 0.2 sub.30
  35.7 0.1 compare_select_fusion
  35.8 2.6 copy.671
  38.4 3.6 reshape.114
  42.0 0.2 and_and_fusion
  42.3 1.7 copy.668
  43.9 1.7 copy.669
  45.7 222.0 %gather_fusion = bf16[65536,128]{1,0:T(8,128)(2,1)} fusion(bf16[32768,128]{1,0:T(8,128)(2,1)} %param.8, s32[65536]{0:T(1024)S(1)} %broadcast_clamp_fusion), kind=kCustom, calls=%fused_computation | custom fusion | bytes 33816576 | tf_op jit(solution)/shard_map/jit(_take)/gather | solution.py:54
  267.7 0.0 copy-start
  267.7 0.0 copy-start.1
  267.7 46.4 %fusion.1 = bf16[8192,128]{1,0:T(8,128)(2,1)S(1)} fusion(bf16[65536,128]{1,0:T(8,128)(2,1)} %gather_fusion, pred[8192,8]{1,0:T(8,128)(4,1)S(1)} %copy.669, pred[8192,8]{1,0:T(8,128)(4,1)S(1)} %copy.668), kind=kLoop, calls=%fused_computation.3 | loop fusion | flops 24117248 | bytes 19005440 | tf_op jit(solution)/shard_map/reduce_sum | solution.py:56
  314.1 1.5 copy.672
  315.6 5.1 %all-to-all-start.1 = ((bf16[128,64,128]{2,1,0:T(8,128)(2,1)}), bf16[128,64,128]{2,1,0:T(8,128)(2,1)S(1)}, u32[]{:S(2)}, u32[]{:S(2)}) async-start(bf16[128,64,128]{2,1,0:T(8,128)(2,1)} %bitcast.548), calls=%async_computation.1 | async-start | bytes 4194304 | tf_op jit(solution)/shard_map/all_to_all | solution.py:60
  320.8 0.0 copy-done
  320.8 0.0 copy-done.1
  320.8 30.1 %all-to-all-done.1 = bf16[128,64,128]{2,1,0:T(8,128)(2,1)S(1)} async-done(((bf16[128,64,128]{2,1,0:T(8,128)(2,1)}), bf16[128,64,128]{2,1,0:T(8,128)(2,1)S(1)}, u32[]{:S(2)}, u32[]{:S(2)}) %all-to-all-start.1) | async-done | bytes 2097184 | tf_op jit(solution)/shard_map/all_to_all | solution.py:60
  350.8 0.4 bitcast_reduce_fusion
  351.2 0.1 copy_bitcast_fusion
  351.3 0.1 broadcast_in_dim.49
  351.4 5.1 %all_to_all.15 = bf16[2,64,4096]{2,1,0:T(8,128)(2,1)S(1)} all-to-all(bf16[2,64,4096]{2,1,0:T(8,128)(2,1)S(1)} %broadcast_in_dim.49), channel_id=1, replica_groups=mesh['section'=2,'dev'=64] {'section'}, dimensions={0} | all-to-all | bytes 2097152 | tf_op jit(solution)/shard_map/all_to_all | solution.py:9
  356.5 0.0 all-gather.4.cloned.1.call-done
  356.5 8.2 %fusion.4 = f32[128]{0:T(128)S(1)} fusion(bf16[128,4096]{1,0:T(8,128)(2,1)S(1)} %bitcast.549, bf16[4096,2048]{1,0:T(8,128)(2,1)} %all-gather.4.cloned.1.call-done, f32[2048]{0:T(1024)S(1)} %convert_element_type.5, f32[2048]{0:T(1024)S(1)} %convert_element_type.4), kind=kOutput, calls=%fused_computation.8 | convolution fusion | flops 2148532224 | bytes 17842688 | tf_op jit(solution)/shard_map/dot_general | solution.py:75
  364.8 1.8 all-gather.1
  366.6 0.5 reduce_sum.55
  (132 shorter events, 0.5 us)
Async XLA Ops:
  6.5 350.0 %all-gather.4.cloned.1.call-start = ((), (), s32[]{:S(2)}) async-start(), calls=%async_computation.3 | async-start | bytes 17039360 | tf_op jit(solution)/shard_map/all_gather | solution.py:74
  10.6 22.3 %all-to-all-start = ((s32[128,1,512]{2,1,0:T(1,128)}), s32[128,1,512]{2,1,0:T(1,128)S(1)}, u32[]{:S(2)}, u32[]{:S(2)}) async-start(s32[128,1,512]{2,1,0:T(1,128)} %reshape.125), calls=%async_computation | async-start | bytes 524288 | tf_op jit(solution)/shard_map/all_to_all | solution.py:41
  267.7 53.1 %copy-start = (bf16[2048]{0:T(1024)(128)(2,1)S(1)}, bf16[2048]{0:T(1024)(128)(2,1)}, u32[]{:S(2)}) copy-start(bf16[2048]{0:T(1024)(128)(2,1)} %param.10) | copy-start | bytes 12292
  267.7 53.1 %copy-start.1 = (bf16[2048]{0:T(1024)(128)(2,1)S(1)}, bf16[2048]{0:T(1024)(128)(2,1)}, u32[]{:S(2)}) copy-start(bf16[2048]{0:T(1024)(128)(2,1)} %param.11) | copy-start | bytes 12292
  315.6 35.2 %all-to-all-start.1 = ((bf16[128,64,128]{2,1,0:T(8,128)(2,1)}), bf16[128,64,128]{2,1,0:T(8,128)(2,1)S(1)}, u32[]{:S(2)}, u32[]{:S(2)}) async-start(bf16[128,64,128]{2,1,0:T(8,128)(2,1)} %bitcast.548), calls=%async_computation.1 | async-start | bytes 4194304 | tf_op jit(solution)/shard_map/all_to_all | solution.py:60
Sparse Core Ops, SparseCore 0:
  10.2 107.6 all-gather.3
